TPU v7x, 8 devices: a whole 2x2x1 slice. The times are simulated.
8 devices in a mesh: mat: 1 (over z), col: 2 (over y), row: 4 (over x, core).
Axes of the slice: x: 2, y: 2, z: 1, core: 2. Of those that a mesh axis runs over, the one named last changes fastest.
Arguments:
- a_mat: float32 [8192, 4, 192], P(('mat', 'row'), 'col')
Outputs:
- output 1: float32 [8192, 4, 192], P(('mat', 'row'), 'col')
- output 2: float32 [4, 192], P(('mat', 'col'))
- output 3: float32 [4, 192, 192], P(('mat', 'col'))
All inputs are finite; a program needn't handle non-finite values.
Results may differ from a plain program's by a relative error of at most 0.001.
Values sent between devices are 32-bit elements.
A program may use at most 1 GiB of HBM per device.

v0:
```python
import jax
import jax.numpy as jnp
from jax import lax
from jax.sharding import PartitionSpec as P

FULL_PREC = lax.Precision.HIGHEST


def factor_panel(panel, row_start, diag_start):
    loc_rows, width = panel.shape
    row_ids = row_start + jnp.arange(loc_rows)[:, None]
    col_ids = jnp.arange(width)

    def col_step(col_k, carry):
        panel_now, tau_vec = carry
        diag_row = diag_start + col_k
        col_x = lax.dynamic_slice_in_dim(panel_now, col_k, 1, axis=1)
        is_below = row_ids > diag_row
        at_diag = row_ids == diag_row
        x_below = jnp.where(is_below, col_x, 0.0)
        pick_rows = jnp.concatenate([at_diag.astype(jnp.float32), x_below], axis=1)
        red_pair = jnp.einsum('rt,rc->tc', pick_rows, panel_now, precision=FULL_PREC, preferred_element_type=jnp.float32)
        red_pair = lax.psum(red_pair, 'row')
        row_k = red_pair[0]
        dot_vals = red_pair[1]
        alpha_val = jnp.sum(jnp.where(col_ids == col_k, row_k, 0.0))
        norm_val = jnp.sqrt(alpha_val * alpha_val + jnp.sum(jnp.where(col_ids == col_k, dot_vals, 0.0)))
        beta_val = jnp.where(alpha_val >= 0.0, -norm_val, norm_val)
        tau_k = (beta_val - alpha_val) / beta_val
        scale_k = 1.0 / (alpha_val - beta_val)
        w_row = jnp.where(col_ids > col_k, row_k + scale_k * dot_vals, 0.0)
        v_col = jnp.where(is_below, col_x * scale_k, at_diag.astype(jnp.float32))
        panel_now = panel_now - (tau_k * v_col) * w_row[None, :]
        new_col = jnp.where(is_below, col_x * scale_k, jnp.where(at_diag, beta_val, col_x))
        panel_now = lax.dynamic_update_slice_in_dim(panel_now, new_col, col_k, axis=1)
        tau_vec = jnp.where(col_ids == col_k, tau_k, tau_vec)
        return panel_now, tau_vec

    return lax.fori_loop(0, width, col_step, (panel, jnp.zeros((width,), jnp.float32)))


def build_t(v_gram, tau_vec):
    width = tau_vec.shape[0]
    col_ids = jnp.arange(width)

    def col_step(col_i, t_mat):
        g_col = lax.dynamic_slice_in_dim(v_gram, col_i, 1, axis=1)[:, 0]
        g_col = jnp.where(col_ids < col_i, g_col, 0.0)
        tau_i = jnp.sum(jnp.where(col_ids == col_i, tau_vec, 0.0))
        t_col = -tau_i * jnp.dot(t_mat, g_col, precision=FULL_PREC, preferred_element_type=jnp.float32)
        t_col = jnp.where(col_ids == col_i, tau_i, t_col)
        return jnp.where(col_ids[None, :] == col_i, t_col[:, None], t_mat)

    return lax.fori_loop(0, width, col_step, jnp.zeros((width, width), jnp.float32))


def solution(mesh):
    col_count = mesh.shape['col']
    spec_a = P(('mat', 'row'), 'col', None)
    spec_tau = P(('mat', 'col'), None)
    spec_t = P(('mat', 'col'), None, None)

    def per_device(a_blk):
        loc_rows, loc_panels, width = a_blk.shape
        me_col = lax.axis_index('col')
        row_start = lax.axis_index('row') * loc_rows
        row_ids = row_start + jnp.arange(loc_rows)[:, None]
        col_ids = jnp.arange(width)[None, :]
        trail_all = a_blk
        done_list = []
        tau_list = []
        t_list = []
        tau_keep = None
        t_keep = None
        for panel_j in range(loc_panels * col_count):
            own_col = panel_j % col_count
            is_owner = me_col == own_col
            head_panel = trail_all[:, 0]
            fac_panel, tau_vec = factor_panel(head_panel, row_start, panel_j * width)
            diag_cols = panel_j * width + col_ids
            v_mat = jnp.where(row_ids > diag_cols, fac_panel, (row_ids == diag_cols).astype(jnp.float32))
            v_gram = lax.psum(jnp.einsum('rk,rl->kl', v_mat, v_mat, precision=FULL_PREC, preferred_element_type=jnp.float32), 'row')
            t_mat = build_t(v_gram, tau_vec)
            packed = jnp.concatenate([v_mat, t_mat], axis=0)
            packed = lax.psum(jnp.where(is_owner, packed, 0.0), 'col')
            v_own = packed[:loc_rows]
            t_own = packed[loc_rows:]
            if own_col == 0:
                tau_keep = jnp.zeros_like(tau_vec)
                t_keep = jnp.zeros_like(t_mat)
            tau_keep = jnp.where(is_owner, tau_vec, tau_keep)
            t_keep = jnp.where(is_owner, t_mat, t_keep)
            last_in_round = own_col == col_count - 1
            if last_in_round:
                region = trail_all[:, 1:]
            else:
                region = trail_all
            if region.shape[1] > 0:
                part_w = jnp.einsum('rk,rsc->ksc', v_own, region, precision=FULL_PREC, preferred_element_type=jnp.float32)
                w_sum = lax.psum(part_w, 'row')
                w_mat = jnp.einsum('kl,ksc->lsc', t_own, w_sum, precision=FULL_PREC, preferred_element_type=jnp.float32)
                if not last_in_round:
                    keep_slot = (jnp.arange(region.shape[1]) > 0) | (me_col > own_col)
                    w_mat = jnp.where(keep_slot[None, :, None], w_mat, 0.0)
                region = region - jnp.einsum('rl,lsc->rsc', v_own, w_mat, precision=FULL_PREC, preferred_element_type=jnp.float32)
            if last_in_round:
                done_list.append(jnp.where(is_owner, fac_panel, head_panel))
                tau_list.append(tau_keep)
                t_list.append(t_keep)
                trail_all = region
            else:
                first_slot = jnp.where(is_owner, fac_panel, region[:, 0])
                trail_all = lax.dynamic_update_slice_in_dim(region, first_slot[:, None, :], 0, axis=1)
        return jnp.stack(done_list, axis=1), jnp.stack(tau_list), jnp.stack(t_list)

    return jax.shard_map(per_device, mesh=mesh, in_specs=(spec_a,), out_specs=(spec_a, spec_tau, spec_t), check_vma=False)
```

profile of v0, /device:TPU:0, one launch (start us, length us, event | category | flops | bytes accessed | tf_op | source)
XLA Modules:
  0.0 12087.8 jit_solution(14914287607938607252)
XLA Ops:
  8.8 2412.1 %while.128 = (s32[]{:T(128)}, f32[2048,192]{0,1:T(8,128)S(1)}, f32[192]{0:T(256)S(1)}, s32[]{:T(128)}, s32[]{:T(128)}, /*index=5*/f32[]{:T(128)}, f32[]{:T(128)}, s32[]{:T(128)}) while((s32[]{:T(128)}, f32[2048,192]{0,1:T(8,128)S(1)}, f32[192]{0:T(256)S(1)}, s32[]{:T(128)}, s32[]{:T(128)}, /*index=5*/f32[]{:T(128)}, ...), condition=%wide.region_4.5_spmd.clone.clone, body=%wide.region_0.4_spmd.clone.clone.sunk | while | flops 10261130 | bytes 4826241 | solution.py:39
  10.1 8.7 psum.136
  137.5 6.5 psum.136
  1757.3 6.5 psum.136
  2208.9 6.5 psum.136
  2423.3 26.4 all-reduce.11.cloned.1.call-done
  2450.7 687.3 %while.129 = (s32[]{:T(128)}, f32[192,192]{1,0:T(8,128)S(1)}, f32[192]{0:T(256)S(1)}, f32[192,192]{0,1:T(8,128)S(1)}, s32[]{:T(128)}, /*index=5*/s32[]{:T(128)}) while((s32[]{:T(128)}, f32[192,192]{1,0:T(8,128)S(1)}, f32[192]{0:T(256)S(1)}, f32[192,192]{0,1:T(8,128)S(1)}, s32[]{:T(128)}, /*index=5*/s32[]{:T(128)}) %tuple.308), condition=%wide.region_8.9_spmd.clone.clone, body=%wide.region_6.8_spmd.clone.clone.sunk | while | flops 554691 | bytes 450548 | solution.py:54
  3139.6 50.1 all-reduce.13.cloned.1.call-done
  3196.8 26.4 all-reduce.15.cloned.1.call-done
  3231.4 2406.8 %while.130 = (s32[]{:T(128)}, f32[2048,192]{0,1:T(8,128)S(1)}, f32[192]{0:T(256)S(1)}, s32[]{:T(128)}, s32[]{:T(128)}, /*index=5*/f32[]{:T(128)}, s32[]{:T(128)}, f32[]{:T(128)}, s32[]{:T(128)}) while((s32[]{:T(128)}, f32[2048,192]{0,1:T(8,128)S(1)}, f32[192]{0:T(256)S(1)}, s32[]{:T(128)}, s32[]{:T(128)}, ...), condition=%wide.region_15.16_spmd.clone.clone, body=%wide.region_11.15_spmd.clone.clone.sunk | while | flops 10261131 | bytes 4823213 | solution.py:39
  3344.7 6.5 psum.137
  4962.8 6.5 psum.137
  5413.9 6.5 psum.137
  5643.4 28.1 all-reduce.17.cloned.1.call-done
  5672.5 449.0 %while.131 = (s32[]{:T(128)}, f32[192,192]{1,0:T(8,128)S(1)}, f32[192]{0:T(256)S(1)}, f32[192,192]{0,1:T(8,128)S(1)}, s32[]{:T(128)}, /*index=5*/s32[]{:T(128)}) while((s32[]{:T(128)}, f32[192,192]{1,0:T(8,128)S(1)}, f32[192]{0:T(256)S(1)}, f32[192,192]{0,1:T(8,128)S(1)}, s32[]{:T(128)}, /*index=5*/s32[]{:T(128)}) %tuple.314), condition=%wide.region_19.20_spmd.clone.clone, body=%wide.region_17.19_spmd.clone.clone.sunk | while | flops 554691 | bytes 450548 | solution.py:54
  6123.0 50.1 all-reduce.19.cloned.1.call-done
  6177.9 25.7 all-reduce.21.cloned.1.call-done
  6209.2 2409.0 %while.132 = (s32[]{:T(128)}, f32[2048,192]{0,1:T(8,128)S(1)}, f32[192]{0:T(256)S(1)}, s32[]{:T(128)}, s32[]{:T(128)}, /*index=5*/f32[]{:T(128)}, s32[]{:T(128)}, f32[]{:T(128)}, s32[]{:T(128)}) while((s32[]{:T(128)}, f32[2048,192]{0,1:T(8,128)S(1)}, f32[192]{0:T(256)S(1)}, s32[]{:T(128)}, s32[]{:T(128)}, ...), condition=%wide.region_26.27_spmd.clone.clone, body=%wide.region_22.26_spmd.clone.clone.sunk | while | flops 10261131 | bytes 4823213 | solution.py:39
  6322.6 6.5 psum.138
  7942.2 6.5 psum.138
  8393.8 6.5 psum.138
  8621.9 26.1 all-reduce.23.cloned.1.call-done
  8649.1 449.1 %while.133 = (s32[]{:T(128)}, f32[192,192]{1,0:T(8,128)S(1)}, f32[192]{0:T(256)S(1)}, f32[192,192]{0,1:T(8,128)S(1)}, s32[]{:T(128)}, /*index=5*/s32[]{:T(128)}) while((s32[]{:T(128)}, f32[192,192]{1,0:T(8,128)S(1)}, f32[192]{0:T(256)S(1)}, f32[192,192]{0,1:T(8,128)S(1)}, s32[]{:T(128)}, /*index=5*/s32[]{:T(128)}) %tuple.320), condition=%wide.region_30.31_spmd.clone.clone, body=%wide.region_28.30_spmd.clone.clone.sunk | while | flops 554691 | bytes 450548 | solution.py:54
  9101.6 49.5 all-reduce.25.cloned.1.call-done
  9155.5 26.2 all-reduce.27.cloned.1.call-done
  9187.8 2410.7 %while.134 = (s32[]{:T(128)}, f32[2048,192]{0,1:T(8,128)S(1)}, f32[192]{0:T(256)S(1)}, s32[]{:T(128)}, s32[]{:T(128)}, /*index=5*/f32[]{:T(128)}, s32[]{:T(128)}, f32[]{:T(128)}, s32[]{:T(128)}) while((s32[]{:T(128)}, f32[2048,192]{0,1:T(8,128)S(1)}, f32[192]{0:T(256)S(1)}, s32[]{:T(128)}, s32[]{:T(128)}, ...), condition=%wide.region_37.38_spmd.clone.clone, body=%wide.region_33.37_spmd.clone.clone.sunk | while | flops 10261131 | bytes 4823213 | solution.py:39
  9301.3 6.5 psum.139
  9778.5 6.5 psum.139
  10922.0 6.5 psum.139
  11373.9 6.5 psum.139
  11608.3 21.7 all-reduce.29.cloned.1.call-done
  11631.1 449.1 %while.135 = (s32[]{:T(128)}, f32[192,192]{1,0:T(8,128)S(1)}, f32[192]{0:T(256)S(1)}, f32[192,192]{0,1:T(8,128)S(1)}, s32[]{:T(128)}, /*index=5*/s32[]{:T(128)}) while((s32[]{:T(128)}, f32[192,192]{1,0:T(8,128)S(1)}, f32[192]{0:T(256)S(1)}, f32[192,192]{0,1:T(8,128)S(1)}, s32[]{:T(128)}, /*index=5*/s32[]{:T(128)}) %tuple.326), condition=%wide.region_41.42_spmd.clone.clone, body=%wide.region_39.41_spmd.clone.clone.sunk | while | flops 554691 | bytes 450548 | solution.py:54
  (13908 shorter events, 7934.7 us)
Async XLA Ops:
  7.2 2442.5 %all-reduce.11.cloned.1.call-start = ((), (), s32[]{:S(2)}) async-start(), calls=%async_computation | async-start | bytes 393216 | tf_op jit(solution)/shard_map/psum | solution.py:82
  2423.2 766.4 %all-reduce.13.cloned.1.call-start = ((), (), s32[]{:S(2)}) async-start(), calls=%async_computation.1 | async-start | bytes 3538944 | tf_op jit(solution)/shard_map/psum | solution.py:85
  3138.0 1.5 copy-start.8
  3139.5 83.7 all-reduce.15.cloned.1.call-start
  3189.6 33.6 copy-start.7
  3196.0 2475.5 %all-reduce.17.cloned.1.call-start = ((), (), s32[]{:S(2)}) async-start(), calls=%async_computation.3 | async-start | bytes 393216 | tf_op jit(solution)/shard_map/psum | solution.py:82
  3225.1 2.7 copy-start.4
  3228.6 1.7 copy-start.2
  3230.2 1.2 copy-start.6
  3231.4 2406.8 %copy-start.11 = (s32[192]{0:T(256)S(1)}, s32[192]{0:T(256)}, u32[]{:S(2)}) copy-start(s32[192]{0:T(256)} %iota_add_fusion.7) | copy-start | bytes 2308
  5643.3 529.8 %all-reduce.19.cloned.1.call-start = ((), (), s32[]{:S(2)}) async-start(), calls=%async_computation.4 | async-start | bytes 3538944 | tf_op jit(solution)/shard_map/psum | solution.py:85
  6123.0 80.7 all-reduce.21.cloned.1.call-start
  6123.0 82.0 copy-start.3
  6177.1 2470.9 %all-reduce.23.cloned.1.call-start = ((), (), s32[]{:S(2)}) async-start(), calls=%async_computation.6 | async-start | bytes 393216 | tf_op jit(solution)/shard_map/psum | solution.py:82
  6208.1 1.2 copy-start.1
  6209.2 2409.0 %copy-start.10 = (s32[192]{0:T(256)S(1)}, s32[192]{0:T(256)}, u32[]{:S(2)}) copy-start(s32[192]{0:T(256)} %iota_add_fusion.6) | copy-start | bytes 2308
  8618.5 1.2 copy-start
  8621.8 529.3 %all-reduce.25.cloned.1.call-start = ((), (), s32[]{:S(2)}) async-start(), calls=%async_computation.7 | async-start | bytes 3538944 | tf_op jit(solution)/shard_map/psum | solution.py:85
  9101.0 0.6 copy-start.9
  9101.0 80.7 all-reduce.27.cloned.1.call-start
  9155.2 2474.8 %all-reduce.29.cloned.1.call-start = ((), (), s32[]{:S(2)}) async-start(), calls=%async_computation.9 | async-start | bytes 393216 | tf_op jit(solution)/shard_map/psum | solution.py:82
  9186.7 1.1 copy-start.5
Sparse Core Ops, SparseCore 0:
  2423.4 26.2 all-reduce.10
  3139.6 49.9 all-reduce.12
  3196.1 27.0 all-reduce.14
  5643.4 27.9 all-reduce.16
  6123.1 49.9 all-reduce.18
  6177.2 26.4 all-reduce.20
  8621.9 26.0 all-reduce.22
  9101.2 49.9 all-reduce.24
  9155.3 26.4 all-reduce.26
  11604.0 26.0 all-reduce.28
where the time goes:
time: 12200 us; the launch traced here: 12100 us
  blocking collectives  4590 us (38%)
  loops' own time  3720 us (30%)
  other arithmetic  1910 us (16%)
  matrix products  1340 us (11%)
  waiting for transfers between devices  330 us (3%)
  local copies, waits for them, and re-layouts  183 us (2%)
    psum x768, blocking collectives, col_step(): red_pair = lax.psum(red_pair, 'row')  4590 us
    another operation x4, loops' own time, factor_panel(): lax.fori_loop(0, width, col_step, (panel, jnp.zeros((width,), jnp.float32)))  3130 us
    dot_general x768, matrix products, col_step(): jnp.einsum('rt,rc->tc', pick_rows, panel_now, precision=FULL_PREC, prefer...  1010 us
    another operation x4, loops' own time, build_t(): lax.fori_loop(0, width, col_step, jnp.zeros((width, width), jnp.float32))  589 us
    select_n x768, other arithmetic, col_step(): g_col = jnp.where(col_ids < col_i, g_col, 0.0)  570 us
    select_n x768, other arithmetic, col_step(): t_col = jnp.where(col_ids == col_i, tau_i, t_col)  498 us
    reduce_sum x768, other arithmetic, col_step(): alpha_val = jnp.sum(jnp.where(col_ids == col_k, row_k, 0.0))  475 us
    dot_general x768, matrix products, col_step(): jnp.dot(t_mat, g_col, precision=FULL_PREC, preferred_element_type=jnp.flo...  289 us

commit v1 on v0

v1 whole, which is shorter than its diff:
```python
import functools

import jax
import jax.numpy as jnp
from jax import lax
from jax.experimental import pallas as pl
from jax.experimental.pallas import tpu as pltpu
from jax.sharding import PartitionSpec as P

FULL_PREC = lax.Precision.HIGHEST
SUB = 64
LANES = 128
MIN_PIVOT = 1e-3
MAX_COEF = 64.0


def dot(a, b, ca=1, cb=0):
    return lax.dot_general(a, b, (((ca,), (cb,)), ((), ())), precision=FULL_PREC, preferred_element_type=jnp.float32)


def factor_block(g, b, r_ref, x_ref):
    n = g.shape[0]
    nt = n // 8
    zero = jnp.zeros((n, LANES - n), jnp.float32)
    eye = (lax.broadcasted_iota(jnp.int32, (n, n), 0) == lax.broadcasted_iota(jnp.int32, (n, n), 1)).astype(jnp.float32)
    gp = jnp.concatenate([g, zero], axis=1)
    bp = jnp.concatenate([b, eye], axis=1)
    gt = [gp[8 * i:8 * i + 8] for i in range(nt)]
    bt = [bp[8 * i:8 * i + 8] for i in range(nt)]
    lane = lax.broadcasted_iota(jnp.int32, (8, LANES), 1)
    row8 = lax.broadcasted_iota(jnp.int32, (8, LANES), 0)
    lane1 = lane[0:1]
    tau_row = jnp.zeros((1, LANES), jnp.float32)
    piv_row = jnp.zeros((1, LANES), jnp.float32)
    sgn_row = jnp.zeros((1, LANES), jnp.float32)
    full = (8, LANES)
    for k in range(n):
        t, r = divmod(k, 8)
        row_g = jnp.broadcast_to(gt[t][r:r + 1, :], full)
        piv = jnp.broadcast_to(gt[t][r:r + 1, k:k + 1], full)
        inv = 1.0 / piv
        root = jnp.sqrt(piv)
        right = lane > k
        here = lane == k
        g_right = jnp.where(right, row_g, 0.0)
        r_right = g_right * (root * inv)
        g_keep = jnp.where(here, 1.0, 0.0) * inv + g_right
        for i in range(nt):
            m = jnp.broadcast_to(gt[i][:, k:k + 1], full) * inv
            new = jnp.where(here, m, gt[i] - m * g_right)
            if i == t:
                new = jnp.where(row8 == r, g_keep, new)
            gt[i] = new
        row_b = jnp.broadcast_to(bt[t][r:r + 1, :], full)
        alpha = jnp.broadcast_to(bt[t][r:r + 1, k:k + 1], full)
        s = jnp.where(alpha >= 0.0, 1.0, -1.0)
        beta = -s * root
        xkk = alpha - beta
        rx = 1.0 / xkk
        r_row = -s * r_right
        x_right = jnp.where(right, row_b - r_row, 0.0)
        x_keep = jnp.where(here, rx, jnp.where(right, x_right, row_b))
        for i in range(nt):
            m = jnp.broadcast_to(bt[i][:, k:k + 1], full) * rx
            new = jnp.where(here, m, bt[i] - m * x_right)
            if i == t:
                new = jnp.where(row8 == r, x_keep, new)
            bt[i] = new
        r_ref[k:k + 1, :] = jnp.where(here, beta, r_row)[0:1]
        x_ref[k:k + 1, :] = jnp.where(here, xkk, x_right)[0:1]
        here1 = lane1 == k
        tau_row = jnp.where(here1, ((beta - alpha) / beta)[0:1], tau_row)
        piv_row = jnp.where(here1, piv[0:1], piv_row)
        sgn_row = jnp.where(here1, beta[0:1], sgn_row)
    mg = jnp.concatenate(gt, axis=0)[:, :n]
    mb = jnp.concatenate(bt, axis=0)[:, :n]
    ri = lax.broadcasted_iota(jnp.int32, (n, n), 0)
    ci = lax.broadcasted_iota(jnp.int32, (n, n), 1)
    x_inv_d = jnp.sum(jnp.where(ri == ci, mb, 0.0), axis=1, keepdims=True)
    g_inv_d = jnp.sum(jnp.where(ri == ci, mg, 0.0), axis=1, keepdims=True)
    x_inv = jnp.where(ri == ci, mb, jnp.where(ri < ci, -mb * x_inv_d, 0.0))
    u_inv = jnp.where(ri == ci, mg, jnp.where(ri < ci, -mg * g_inv_d, 0.0))
    r_inv = u_inv * sgn_row[:, :n]
    v = jnp.where(ri > ci, mb, 0.0)
    return v, x_inv, r_inv, tau_row[:, :n], piv_row[:, :n]


def factor_kernel(count, width, g_in, w_in, top_ref, xi_ref, t_ref, tau_ref, ok_ref, g_ref, w_ref, x_ref, rb_ref, xb_ref, gs, bs, ri_s, vi_s, xi_s, rs, xs, vs):
    subs = width // SUB
    ri = lax.broadcasted_iota(jnp.int32, (width, width), 0)
    ci = lax.broadcasted_iota(jnp.int32, (width, width), 1)
    g_ref[...] = g_in[...]
    w_ref[...] = w_in[...]
    xi_ref[...] = jnp.zeros_like(xi_ref)
    top_ref[...] = jnp.zeros_like(top_ref)

    def panel(j, bad):
        gs[...] = g_ref[j, j]
        bs[...] = w_ref[j, j]
        diag0 = jnp.sum(jnp.where(ri == ci, g_in[j, j], 0.0), axis=0, keepdims=True)
        for ref in (rs, xs, vs, ri_s, vi_s, xi_s):
            ref[...] = jnp.zeros_like(ref)
        for s in range(subs):
            c0, c1 = s * SUB, (s + 1) * SUB
            v, x_inv, r_inv, tau, piv = factor_block(gs[c0:c1, c0:c1], bs[c0:c1, c0:c1], rb_ref, xb_ref)
            v_inv = xb_ref[:, SUB:2 * SUB]
            rs[c0:c1, c0:c1] = rb_ref[:, :SUB]
            xs[c0:c1, c0:c1] = xb_ref[:, :SUB]
            vs[c0:c1, c0:c1] = v
            ri_s[c0:c1, c0:c1] = r_inv
            xi_s[c0:c1, c0:c1] = x_inv
            vi_s[c0:c1, c0:c1] = v_inv
            tau_ref[j, 0:1, c0:c1] = tau
            bad = jnp.maximum(bad, jnp.max(jnp.where(piv > MIN_PIVOT * diag0[:, c0:c1], 0.0, 1.0)))
            if s + 1 < subs:
                r_row = dot(r_inv, gs[c0:c1, c1:], 0, 0)
                x_row = dot(v_inv, bs[c0:c1, c1:] - r_row)
                v_col = dot(bs[c1:, c0:c1], x_inv)
                rs[c0:c1, c1:] = r_row
                xs[c0:c1, c1:] = x_row
                vs[c1:, c0:c1] = v_col
                gs[c1:, c1:] -= dot(r_row, r_row, 0, 0)
                bs[c1:, c1:] -= dot(v_col, x_row)
            if s > 0:
                xi_s[:c0, c0:c1] = -dot(xi_s[:c0, :c0], dot(xs[:c0, c0:c1], x_inv))
                ri_s[:c0, c0:c1] = -dot(ri_s[:c0, :c0], dot(rs[:c0, c0:c1], r_inv))
                vi_s[c0:c1, :c0] = -dot(dot(v_inv, vs[c0:c1, :c0]), vi_s[:c0, :c0])
        x_inv, r_inv, v_inv = xi_s[...], ri_s[...], vi_s[...]
        xi_ref[j, j] = x_inv
        top_ref[j, j] = rs[...] + vs[...]
        t_ref[j] = -dot(dot(xs[...], r_inv), v_inv, 1, 1)

        def right(t, carry):
            r_row = dot(r_inv, g_ref[j, t], 0, 0)
            top_ref[j, t] = r_row
            x_ref[j, t] = dot(v_inv, w_ref[j, t] - r_row)
            return carry

        lax.fori_loop(j + 1, count, right, 0)

        def below(i, carry):
            v_col = dot(w_ref[i, j], x_inv)
            top_ref[i, j] = v_col

            def upd_w(t, c):
                w_ref[i, t] -= dot(v_col, x_ref[j, t])
                return c

            lax.fori_loop(j + 1, count, upd_w, 0)
            r_i = top_ref[j, i]

            def upd_g(t, c):
                g_ref[i, t] -= dot(r_i, top_ref[j, t], 0, 0)
                return c

            lax.fori_loop(i, count, upd_g, 0)
            return carry

        lax.fori_loop(j + 1, count, below, 0)

        def inv_col(i, carry):
            def add(m, acc):
                return acc + dot(xi_ref[i, m], x_ref[m, j])

            xi_ref[i, j] = -dot(lax.fori_loop(i, j, add, jnp.zeros((width, width), jnp.float32)), x_inv)
            return carry

        lax.fori_loop(0, j, inv_col, 0)

        def coef(i, acc):
            dcol = jnp.sum(jnp.where(ri == ci, g_in[i, i], 0.0), axis=1, keepdims=True)
            return acc + jnp.sum(jnp.sqrt(dcol) * jnp.abs(xi_ref[i, j]), axis=0, keepdims=True)

        size = lax.fori_loop(0, j + 1, coef, jnp.zeros((1, width), jnp.float32))
        return jnp.maximum(bad, jnp.max(jnp.where(size < MAX_COEF, 0.0, 1.0)))

    bad = lax.fori_loop(0, count, panel, jnp.float32(0.0))
    ok_ref[...] = jnp.full(ok_ref.shape, bad, jnp.float32)


def factor_call(g, w):
    count, width = g.shape[0], g.shape[-1]
    f32 = jnp.float32
    blocks = jax.ShapeDtypeStruct((count, count, width, width), f32)
    vmem = pl.BlockSpec(memory_space=pltpu.VMEM)
    sq = pltpu.VMEM((width, width), f32)
    return pl.pallas_call(
        functools.partial(factor_kernel, count, width),
        out_shape=(blocks, blocks, jax.ShapeDtypeStruct((count, width, width), f32), jax.ShapeDtypeStruct((count, 1, width), f32), jax.ShapeDtypeStruct((8, 128), f32)),
        in_specs=[vmem] * 2,
        out_specs=(vmem,) * 5,
        scratch_shapes=[
            pltpu.VMEM((count, count, width, width), f32),
            pltpu.VMEM((count, count, width, width), f32),
            pltpu.VMEM((count, count, width, width), f32),
            pltpu.VMEM((SUB, LANES), f32),
            pltpu.VMEM((SUB, LANES), f32),
        ] + [sq] * 8,
        compiler_params=pltpu.CompilerParams(vmem_limit_bytes=60 * 1024 * 1024),
    )(g, w)


def factor_panel(panel, row_start, diag_start):
    loc_rows, width = panel.shape
    row_ids = row_start + jnp.arange(loc_rows)[:, None]
    col_ids = jnp.arange(width)

    def col_step(col_k, carry):
        panel_now, tau_vec = carry
        diag_row = diag_start + col_k
        col_x = lax.dynamic_slice_in_dim(panel_now, col_k, 1, axis=1)
        is_below = row_ids > diag_row
        at_diag = row_ids == diag_row
        x_below = jnp.where(is_below, col_x, 0.0)
        pick_rows = jnp.concatenate([at_diag.astype(jnp.float32), x_below], axis=1)
        red_pair = jnp.einsum('rt,rc->tc', pick_rows, panel_now, precision=FULL_PREC, preferred_element_type=jnp.float32)
        red_pair = lax.psum(red_pair, 'row')
        row_k = red_pair[0]
        dot_vals = red_pair[1]
        alpha_val = jnp.sum(jnp.where(col_ids == col_k, row_k, 0.0))
        norm_val = jnp.sqrt(alpha_val * alpha_val + jnp.sum(jnp.where(col_ids == col_k, dot_vals, 0.0)))
        beta_val = jnp.where(alpha_val >= 0.0, -norm_val, norm_val)
        tau_k = (beta_val - alpha_val) / beta_val
        scale_k = 1.0 / (alpha_val - beta_val)
        w_row = jnp.where(col_ids > col_k, row_k + scale_k * dot_vals, 0.0)
        v_col = jnp.where(is_below, col_x * scale_k, at_diag.astype(jnp.float32))
        panel_now = panel_now - (tau_k * v_col) * w_row[None, :]
        new_col = jnp.where(is_below, col_x * scale_k, jnp.where(at_diag, beta_val, col_x))
        panel_now = lax.dynamic_update_slice_in_dim(panel_now, new_col, col_k, axis=1)
        tau_vec = jnp.where(col_ids == col_k, tau_k, tau_vec)
        return panel_now, tau_vec

    return lax.fori_loop(0, width, col_step, (panel, jnp.zeros((width,), jnp.float32)))


def build_t(v_gram, tau_vec):
    width = tau_vec.shape[0]
    col_ids = jnp.arange(width)

    def col_step(col_i, t_mat):
        g_col = lax.dynamic_slice_in_dim(v_gram, col_i, 1, axis=1)[:, 0]
        g_col = jnp.where(col_ids < col_i, g_col, 0.0)
        tau_i = jnp.sum(jnp.where(col_ids == col_i, tau_vec, 0.0))
        t_col = -tau_i * jnp.dot(t_mat, g_col, precision=FULL_PREC, preferred_element_type=jnp.float32)
        t_col = jnp.where(col_ids == col_i, tau_i, t_col)
        return jnp.where(col_ids[None, :] == col_i, t_col[:, None], t_mat)

    return lax.fori_loop(0, width, col_step, jnp.zeros((width, width), jnp.float32))


def column_plan(a_blk, col_count):
    loc_rows, loc_panels, width = a_blk.shape
    me_col = lax.axis_index('col')
    row_start = lax.axis_index('row') * loc_rows
    row_ids = row_start + jnp.arange(loc_rows)[:, None]
    col_ids = jnp.arange(width)[None, :]
    slots = jnp.arange(loc_panels)

    def step(panel_j, carry):
        work, tau_all, t_all = carry
        own_col = panel_j % col_count
        slot = panel_j // col_count
        is_owner = me_col == own_col
        head = lax.dynamic_slice_in_dim(work, slot, 1, axis=1)[:, 0]
        fac, tau_vec = factor_panel(head, row_start, panel_j * width)
        diag_cols = panel_j * width + col_ids
        v_mat = jnp.where(row_ids > diag_cols, fac, (row_ids == diag_cols).astype(jnp.float32))
        v_gram = lax.psum(jnp.einsum('rk,rl->kl', v_mat, v_mat, precision=FULL_PREC, preferred_element_type=jnp.float32), 'row')
        t_mat = build_t(v_gram, tau_vec)
        packed = lax.psum(jnp.where(is_owner, jnp.concatenate([v_mat, t_mat], axis=0), 0.0), 'col')
        v_own, t_own = packed[:loc_rows], packed[loc_rows:]
        w_sum = lax.psum(jnp.einsum('rk,rsc->ksc', v_own, work, precision=FULL_PREC, preferred_element_type=jnp.float32), 'row')
        w_mat = jnp.einsum('kl,ksc->lsc', t_own, w_sum, precision=FULL_PREC, preferred_element_type=jnp.float32)
        later = slots * col_count + me_col > panel_j
        w_mat = jnp.where(later[None, :, None], w_mat, 0.0)
        new = work - jnp.einsum('rl,lsc->rsc', v_own, w_mat, precision=FULL_PREC, preferred_element_type=jnp.float32)
        mine = is_owner & (slots == slot)
        work = jnp.where(mine[None, :, None], fac[:, None, :], jnp.where(later[None, :, None], new, work))
        tau_all = jnp.where(mine[:, None], tau_vec[None], tau_all)
        t_all = jnp.where(mine[:, None, None], t_mat[None], t_all)
        return work, tau_all, t_all

    init = (a_blk, jnp.zeros((loc_panels, width), jnp.float32), jnp.zeros((loc_panels, width, width), jnp.float32))
    return lax.fori_loop(0, loc_panels * col_count, step, init)


def solution(mesh):
    col_count = mesh.shape['col']
    spec_a = P(('mat', 'row'), 'col', None)
    spec_tau = P(('mat', 'col'), None)
    spec_t = P(('mat', 'col'), None, None)

    def per_device(a_blk):
        loc_rows, loc_panels, width = a_blk.shape
        count = loc_panels * col_count
        total = count * width
        me_col = lax.axis_index('col')
        me_row = lax.axis_index('row')
        full = lax.all_gather(a_blk, 'col', axis=1, tiled=True)
        order = [(j % col_count) * loc_panels + j // col_count for j in range(count)]
        a_all = jnp.concatenate([full[:, o] for o in order], axis=1)
        gram = jnp.einsum('rk,rl->kl', a_all, a_all, precision=FULL_PREC, preferred_element_type=jnp.float32)
        head = jnp.where(me_row == 0, a_all[:total], 0.0)
        both = lax.psum(jnp.stack([gram, head]), 'row')
        blocks = both.reshape(2, count, width, count, width).transpose(0, 1, 3, 2, 4)
        top, x_inv, t_mat, tau, bad = factor_call(blocks[0], blocks[1])

        def own(x, axis):
            picks = [lax.dynamic_slice_in_dim(x, s * col_count + me_col, 1, axis=axis) for s in range(loc_panels)]
            return jnp.concatenate(picks, axis=axis)

        def gram_plan(a_blk):
            xi_own = own(x_inv, 1).transpose(0, 2, 1, 3).reshape(total, loc_panels * width)
            top_own = own(top, 1).transpose(0, 2, 1, 3).reshape(total, loc_panels, width)
            v_all = jnp.dot(a_all, xi_own, precision=FULL_PREC, preferred_element_type=jnp.float32).reshape(loc_rows, loc_panels, width)
            head_rows = jnp.where(me_row == 0, top_own, v_all[:total])
            return jnp.concatenate([head_rows, v_all[total:]], axis=0), own(tau[:, 0], 0), own(t_mat, 0)

        def safe_plan(a_blk):
            return column_plan(a_blk, col_count)

        return lax.cond(bad[0, 0] < 0.5, gram_plan, safe_plan, a_blk)

    return jax.shard_map(per_device, mesh=mesh, in_specs=(spec_a,), out_specs=(spec_a, spec_tau, spec_t), check_vma=False)
```

time: 12200 us -> 477 us (0.04)
  blocking collectives: 4590 us -> 0 us
  loops' own time: 3720 us -> 0.88 us
  other arithmetic: 1910 us -> 13.8 us
  matrix products: 1340 us -> 36 us
  Pallas kernels: 0 us -> 153 us
  waiting for transfers between devices: 330 us -> 195 us
  local copies, waits for them, and re-layouts: 183 us -> 59.1 us
    psum x768 -> x0, blocking collectives: 4590 us -> none  [col_step(): red_pair = lax.psum(red_pair, 'row')]
    another operation x8 -> x1, loops' own time: 3720 us -> 0.88 us  [per_device(): return lax.cond(bad[0, 0] < 0.5, gram_plan, safe_plan, a_blk)]
    dot_general x1548 -> x2, matrix products: 1330 us -> 36 us  [the longest x1 18.5 us: per_device(): jnp.einsum('rk,rl->kl', a_all, a_all, precision=FULL_PREC, preferred_elem...]
    select_n x5384 -> x1, other arithmetic: 1210 us -> 1.55 us  [gram_plan(): head_rows = jnp.where(me_row == 0, top_own, v_all[:total])]
    reduce_sum x768 -> x0, other arithmetic: 475 us -> none  [col_step(): alpha_val = jnp.sum(jnp.where(col_ids == col_k, row_k, 0.0))]
    psum x10 -> x1, waiting for transfers between devices: 330 us -> 114 us  [per_device(): both = lax.psum(jnp.stack([gram, head]), 'row')]
    sub x769 -> x0, other arithmetic: 201 us -> none  [the longest x768 200 us: col_step(): panel_now = panel_now - tau_k * v_col * w_row[None, :]]
    dynamic_update_slice x768 -> x0, local copies, waits for them, and re-layouts: 157 us -> none  [col_step(): lax.dynamic_update_slice_in_dim(panel_now, new_col, col_k, axis=1)]
where the time goes in v1:
time: 477 us; the launch traced here: 474 us
  waiting for transfers between devices  195 us (41%)
  Pallas kernels  153 us (32%)
  local copies, waits for them, and re-layouts  59.1 us (12%)
  matrix products  36 us (8%)
  between operations  15 us (3%)
  other arithmetic  13.8 us (3%)
    pallas_call x1, Pallas kernels, factor_call(): pl.pallas_call(functools.partial(factor_kernel, count, width), out_shape=...  153 us
    psum x1, waiting for transfers between devices, per_device(): both = lax.psum(jnp.stack([gram, head]), 'row')  114 us
    all_gather x1, waiting for transfers between devices, per_device(): full = lax.all_gather(a_blk, 'col', axis=1, tiled=True)  81.2 us
    dot_general x1, matrix products, per_device(): jnp.einsum('rk,rl->kl', a_all, a_all, precision=FULL_PREC, preferred_elem...  18.5 us
    dot_general x1, matrix products, gram_plan(): jnp.dot(a_all, xi_own, precision=FULL_PREC, preferred_element_type=jnp.fl...  17.5 us
    reshape x2, local copies, waits for them, and re-layouts, per_device(): both.reshape(2, count, width, count, width).transpose(0, 1, 3, 2, 4)  14.7 us
    unnamed x7, local copies, waits for them, and re-layouts  14.2 us
  transfers between devices with their start and end apart: 2, of which 2 were waited for; matrix products, arithmetic and copies ran while one was open for 0% of the time, Pallas kernels for 0%

profile of v1, /device:TPU:0, one launch (start us, length us, event | category | flops | bytes accessed | tf_op | source)
XLA Modules:
  0.0 473.5 jit_solution(9276743548659881887)
XLA Ops:
  7.2 3.9 copy.77
  11.2 81.2 %all-gather.2.cloned.1.call-done = f32[2048,4,192]{0,2,1:T(8,128)} async-done(((f32[2048,2,192]{0,2,1:T(8,128)}), f32[2048,4,192]{0,2,1:T(8,128)}) %all-gather.2.cloned.1.call-update) | async-done | bytes 6291472 | tf_op jit(solution)/shard_map/all_gather | solution.py:299
  92.4 5.7 %fusion.41 = (f32[2048,1,192]{0,2,1:T(8,128)}, f32[2048,1,192]{0,2,1:T(8,128)}, f32[2048,1,192]{0,2,1:T(8,128)}, f32[2048,1,192]{0,2,1:T(8,128)}) fusion(f32[2048,4,192]{0,2,1:T(8,128)} %all-gather.2.cloned.1.call-done), kind=kLoop, calls=%fused_computation.85 | loop fusion | bytes 12582912 | tf_op jit(solution)/shard_map/slice | solution.py:301
  98.1 1.8 copy.26
  99.9 2.8 copy.28
  102.7 2.8 copy.27
  105.6 2.8 copy.29
  108.4 4.4 pad_maximum_fusion.3
  112.8 18.5 %convolution_bitcast_fusion.1 = f32[1,768,768]{2,1,0:T(8,128)S(1)} fusion(f32[2048,768]{1,0:T(8,128)S(1)} %pad_maximum_fusion.3), kind=kOutput, calls=%fused_computation.83 | convolution fusion | flops 14495514624 | bytes 8650752 | tf_op jit(solution)/shard_map/rk,rl->kl/dot_general | solution.py:302
  131.5 2.4 pad_maximum_fusion.4
  133.9 8.2 %reshape.118 = f32[2,4,192,4,192]{4,3,2,1,0:T(4,128)} reshape(f32[2,768,768]{2,1,0:T(8,128)} %pad_maximum_fusion.4) | data formatting | bytes 9437184 | tf_op jit(solution)/shard_map/reshape | solution.py:305
  142.1 6.5 %copy.31 = f32[2,4,192,4,192]{4,2,3,1,0:T(8,128)} copy(f32[2,4,192,4,192]{4,3,2,1,0:T(4,128)} %reshape.118) | data formatting | bytes 9437184 | tf_op jit(solution)/shard_map/reshape | solution.py:305
  148.6 114.0 %all-reduce.5.cloned.1.call-done = f32[2,4,4,192,192]{4,3,2,1,0:T(8,128)} async-done(((f32[2,4,4,192,192]{4,3,2,1,0:T(8,128)}), f32[2,4,4,192,192]{4,3,2,1,0:T(8,128)}) %all-reduce.5.cloned.1.call-update) | async-done | bytes 4718608 | tf_op jit(solution)/shard_map/psum | solution.py:304
  262.5 6.1 %slice_bitcast_fusion.2 = (f32[4,4,192,192]{3,2,1,0:T(8,128)}, f32[4,4,192,192]{3,2,1,0:T(8,128)}) fusion(f32[2,4,4,192,192]{4,3,2,1,0:T(8,128)} %all-reduce.5.cloned.1.call-done), kind=kLoop, calls=%fused_computation.79 | loop fusion | bytes 9437184 | tf_op jit(solution)/shard_map/squeeze | solution.py:306
  268.7 153.5 %shard_map.41 = (f32[4,4,192,192]{3,2,1,0:T(8,128)}, f32[4,4,192,192]{3,2,1,0:T(8,128)}, f32[4,192,192]{2,1,0:T(8,128)}, f32[4,1,192]{2,1,0:T(1,128)}, f32[8,128]{1,0:T(8,128)}) custom-call(f32[4,4,192,192]{3,2,1,0:T(8,128)} %get-tuple-element.794.g_in, f32[4,4,192,192]{3,2,1,0:T(8,128)} %get-tuple-element.793.w_in), custom_call_target="tpu_custom_call" | custom-call | tf_op jit(solution)/shard_map/pallas_call | solution.py:187
  422.1 1.2 slice.77
  424.0 42.4 %conditional.1 = (f32[2048,2,192]{0,2,1:T(8,128)}, f32[2,192]{1,0:T(2,128)}, f32[2,192,192]{2,1,0:T(8,128)}) conditional(s32[]{:T(128)} %bitcast.16, f32[2048,2,192]{0,2,1:T(8,128)} %copy.77, (s32[]{:T(128)}, s32[]{:T(128)}, f32[4,4,192,192]{3,2,1,0:T(8,128)}, f32[4,4,192,192]{3,2,1,0:T(8,128)}, f32[2048,768]{1,0:T(8,128)}, ...), branch_computations={%region_1.15_spmd, %region_15.16_spmd} | conditional | flops 7249502720 | bytes 85912464 | solution.py:322
  424.6 1.1 constant_dynamic-slice_fusion.1
  425.7 0.8 pad_maximum_fusion.1
  426.4 0.7 fusion.12
  427.1 0.6 pad_maximum_fusion.2
  427.7 3.9 copy.25
  431.6 1.4 constant_dynamic-slice_fusion.5
  433.0 1.6 maximum_bitcast_fusion.1
  434.6 2.3 reshape.116
  437.0 17.5 %convolution_bitcast_fusion = f32[2048,384]{0,1:T(8,128)S(1)} fusion(f32[768,384]{1,0:T(8,128)} %reshape.116, f32[2048,768]{1,0:T(8,128)} %get-tuple-element.487), kind=kOutput, calls=%fused_computation.7 | convolution fusion | flops 7247757312 | bytes 10616832 | tf_op jit(solution)/shard_map/cond/branch_1_fun/dot_general | solution.py:315
  454.4 1.6 copy-done.4
  456.1 3.5 copy.24
  459.8 0.4 maximum_bitcast_fusion
  460.2 2.0 reshape.115
  462.3 1.6 broadcast_select_fusion
  464.2 2.0 pad_maximum_fusion
  (13 shorter events, 0.9 us)
Async XLA Ops:
  7.2 85.2 %all-gather.2.cloned.1.call-start = ((), (), s32[]{:S(2)}) async-start(), calls=%async_computation | async-start | bytes 9437184 | tf_op jit(solution)/shard_map/all_gather | solution.py:299
  11.1 251.4 %all-reduce.5.cloned.1.call-start = ((), (), s32[]{:S(2)}) async-start(), calls=%async_computation.1 | async-start | bytes 12582912 | tf_op jit(solution)/shard_map/psum | solution.py:304
  112.8 18.5 %copy-start.3 = (f32[2048,768]{1,0:T(8,128)}, f32[2048,768]{1,0:T(8,128)S(1)}, u32[]{:S(2)}) copy-start(f32[2048,768]{1,0:T(8,128)S(1)} %pad_maximum_fusion.3) | copy-start | bytes 18874372
  454.4 1.6 copy-start.4
  460.2 2.1 slice-start
  462.3 1.9 slice-start.1
Sparse Core Ops, SparseCore 0:
  11.3 81.0 all-gather.1
  148.7 113.7 all-reduce.4
